TPU v7x, 32 devices: a whole 2x2x4 slice. The times are simulated.
32 devices in a mesh: clip: 4 (over y, core), frame: 2 (over x), pix: 4 (over z).
Axes of the slice: x: 2, y: 2, z: 4, core: 2. Of those that a mesh axis runs over, the one named last changes fastest.
Arguments:
- features: bfloat16 [8, 8, 96, 256], P(('clip', 'frame'), 'pix'), parts along dimension 0, may hold values from -6 to 6
Outputs:
- forward_full: bfloat16 [8, 8, 96, 768], P(('clip', 'frame'), 'pix'), parts along dimension 0
- forward_half: bfloat16 [8, 8, 96, 192], P(('clip', 'frame'), 'pix'), parts along dimension 0
- forward_quarter: bfloat16 [8, 8, 96, 48], P(('clip', 'frame'), 'pix'), parts along dimension 0
- forward_eighth: bfloat16 [8, 8, 96, 12], P(('clip', 'frame'), 'pix'), parts along dimension 0
- backward_full: bfloat16 [8, 8, 96, 768], P(('clip', 'frame'), 'pix'), parts along dimension 0
- backward_half: bfloat16 [8, 8, 96, 192], P(('clip', 'frame'), 'pix'), parts along dimension 0
- backward_quarter: bfloat16 [8, 8, 96, 48], P(('clip', 'frame'), 'pix'), parts along dimension 0
- backward_eighth: bfloat16 [8, 8, 96, 12], P(('clip', 'frame'), 'pix'), parts along dimension 0
There are 4 independent parts, one for each index of `clip`. A program takes and returns all parts, laid end to end along the dimension named above; each array names one. Nothing has to cross between parts.
All inputs are finite; a program needn't handle non-finite values.
Results may differ from a plain program's by a relative error of at most 0.001.
Values may be sent and summed in bfloat16 or wider, within the bound.
No kernel may reach another device: no remote copies, remote signals or barrier semaphores. Data moves between devices by JAX's collectives and lax.ppermute only.
A program may use at most 64 MiB of HBM per device.

v0:
```python
import functools
import math

import jax
import jax.numpy as jnp
from jax import lax
from jax.experimental import pallas as pl
from jax.experimental.pallas import tpu as pltpu
from jax.sharding import PartitionSpec as P


LEVELS = 4
LANES = 128


def from_behind(value, axis, steps):
    count = lax.axis_size(axis)
    leading, last = (max(0, -steps), min(count, count - steps))
    return lax.ppermute(value, axis, [(source, source + steps) for source in range(leading, last)])


def halved(current):
    count, height, breadth = current.shape
    return current.reshape(count, height // 2, 2, breadth // 2, 2).mean(axis=(2, 4))


def pyramid_of(scores, row_count, breadth):
    height = scores.shape[1] // breadth
    current = scores.reshape(scores.shape[0], height, breadth)
    result = []
    for depth_index in range(LEVELS):
        result.append(current.reshape(1, row_count, breadth, -1).astype(jnp.bfloat16))
        if depth_index < LEVELS - 1:
            current = halved(current)
    return result


def many_frames(features):
    row_count, breadth, channels = features.shape[1:]
    own_pixels = features.reshape(row_count * breadth, channels)
    factor = 1.0 / math.sqrt(channels)
    result = []
    for steps in (-1, 1):
        neighbour = from_behind(own_pixels, "frame", steps)
        target = lax.all_gather(neighbour, "pix", axis=0, tiled=True)
        product = lax.dot_general(
            own_pixels, target, (((1,), (1,)), ((), ())), preferred_element_type=jnp.float32
        )
        result += pyramid_of(product * factor, row_count, breadth)
    return tuple(result)


def dot_nt(left, right):
    return lax.dot_general(left, right, (((1,), (1,)), ((), ())), preferred_element_type=jnp.float32)


def by_frame(first, second):
    frame = lax.axis_index("frame")
    pl.when(frame == 0)(first)
    pl.when(frame != 0)(second)


def copy_of(source, target, sems, level):
    return pltpu.make_async_copy(source, target, sems.at[level])


def blank_kernel(features_ref, own_ref, *refs):
    outs, (*blanks, sems, own_sem) = refs[: 2 * LEVELS], refs[2 * LEVELS :]
    forward, backward = outs[:LEVELS], outs[LEVELS:]
    fetch = pltpu.make_async_copy(features_ref, own_ref, own_sem)
    fetch.start()
    for blank in blanks:
        blank[...] = jnp.zeros_like(blank)

    def fill(targets):
        def start():
            for level in range(LEVELS):
                copy_of(blanks[level], targets[level], sems, level).start()

        return start

    by_frame(fill(backward), fill(forward))
    for level in range(LEVELS):
        copy_of(blanks[level], backward[level], sems, level).wait()
    fetch.wait()


def pair_kernel(pix_count, rows, breadth, channels, own_ref, *refs):
    origins = origins_of(pix_count)
    shards, refs = refs[: len(origins)], refs[len(origins) + 2 * LEVELS :]
    outs, (target, summed, pool1, pool2, *values, sems) = refs[: 2 * LEVELS], refs[2 * LEVELS :]
    forward, backward = outs[:LEVELS], outs[LEVELS:]
    v0, v1, v2, v3 = values
    pix = lax.axis_index("pix")
    shard = rows * breadth
    height = rows * pix_count
    factor = 1.0 / math.sqrt(channels)

    def send(level):
        def start(targets):
            return lambda: copy_of(values[level], targets[level], sems, level).start()

        by_frame(start(forward), start(backward))

    for ref, origin in zip(shards, origins):
        place = sum(jnp.where(pix == q, p, 0) for q, p in enumerate(origin))
        target[pl.ds(pl.multiple_of(place * shard, shard), shard), :] = ref[...]

    for r in range(rows):
        scores = dot_nt(own_ref[r * breadth : (r + 1) * breadth, :], target[...]) * factor
        v0[r] = scores.astype(v0.dtype)
    send(0)

    def pooled(load, height, breadth):
        half = breadth // 2
        lines = []
        for i in range(height // 2):
            line = load(2 * i) + load(2 * i + 1)
            for c in range(channels // LANES):
                summed[c, i * breadth : (i + 1) * breadth, :] = line[:, c * LANES : (c + 1) * LANES]
        for i in range(height // 2):
            parts = []
            for c in range(channels // LANES):
                even = summed[c, pl.ds(i * breadth, half, stride=2), :]
                odd = summed[c, pl.ds(i * breadth + 1, half, stride=2), :]
                parts.append((even + odd) * 0.25)
            lines.append(jnp.concatenate(parts, axis=1))
        return jnp.concatenate(lines, axis=0)

    def split(value):
        high = value.astype(jnp.bfloat16)
        return high, (value - high.astype(jnp.float32)).astype(jnp.bfloat16)

    level1 = pooled(lambda i: target[i * breadth : (i + 1) * breadth, :].astype(jnp.float32), height, breadth)
    pool1[...] = level1
    b1 = breadth // 2
    level2 = pooled(lambda i: pool1[i * b1 : (i + 1) * b1, :], height // 2, b1)
    pool2[...] = level2
    b2 = breadth // 4
    level3 = pooled(lambda i: pool2[i * b2 : (i + 1) * b2, :], height // 4, b2)

    high, low = split(level1)
    for r in range(rows):
        own = own_ref[r * breadth : (r + 1) * breadth, :]
        v1[r] = ((dot_nt(own, high) + dot_nt(own, low)) * factor).astype(v1.dtype)
    send(1)
    high, low = split(level2)
    for r in range(rows):
        own = own_ref[r * breadth : (r + 1) * breadth, :]
        v2[r] = ((dot_nt(high, own) + dot_nt(low, own)) * factor).astype(v2.dtype)
    send(2)
    high, low = split(level3)
    lines = []
    for r in range(rows):
        own = own_ref[r * breadth : (r + 1) * breadth, :]
        lines.append((dot_nt(high, own) + dot_nt(low, own)) * factor)
    v3[...] = jnp.stack(lines, axis=1).astype(v3.dtype)
    send(3)
    for level in range(LEVELS):
        copy_of(values[level], forward[level], sems, level).wait()


def rounds_of(pix_count):
    if pix_count == 4:
        return [[2, 0, 3, 1], [1, 3, 0, 2], [0, 2, 1, 3]], True
    return [[p ^ k for p in range(pix_count)] for k in range(pix_count)], False


def origins_of(pix_count):
    rounds, relayed = rounds_of(pix_count)
    origins = [[row.index(q) for q in range(pix_count)] for row in rounds]
    return origins + ([[rounds[0].index(q ^ 1) for q in range(pix_count)]] if relayed else [])


def exchange(own, pix_count):
    rounds, relayed = rounds_of(pix_count)
    got = []
    for row in rounds:
        pairs = [(f * pix_count + p, (1 - f) * pix_count + row[p]) for f in range(2) for p in range(pix_count)]
        got.append(lax.ppermute(own, ("frame", "pix"), pairs))
    if relayed:
        got.append(lax.ppermute(got[0], "pix", [(p, p ^ 1) for p in range(pix_count)]))
    return got


def two_frames(features):
    rows, breadth, channels = features.shape[1:]
    pix_count = lax.axis_size("pix")
    shard = rows * breadth
    pixels = shard * pix_count
    own = features.reshape(shard, channels)
    shards = exchange(own, pix_count)
    count = len(shards)

    shapes = [
        (rows, breadth, pixels),
        (rows, breadth, pixels // 4),
        (rows, pixels // 16, breadth),
        (pixels // 64, rows, breadth),
    ]
    vmem = pl.BlockSpec(memory_space=pltpu.VMEM)
    anywhere = pl.BlockSpec(memory_space=pl.ANY)
    out_shapes = [jax.ShapeDtypeStruct(s, jnp.bfloat16) for s in shapes * 2]
    staging = [pltpu.VMEM(s, jnp.bfloat16) for s in shapes]
    limits = pltpu.CompilerParams(vmem_limit_bytes=16 * 2**20)
    near, *blanks = pl.pallas_call(
        blank_kernel,
        out_shape=[jax.ShapeDtypeStruct(own.shape, own.dtype)] + out_shapes,
        in_specs=[anywhere],
        out_specs=[vmem] + [anywhere] * (2 * LEVELS),
        scratch_shapes=staging + [pltpu.SemaphoreType.DMA((LEVELS,)), pltpu.SemaphoreType.DMA],
        compiler_params=limits,
        cost_estimate=pl.CostEstimate(flops=shard * pixels * channels, bytes_accessed=4 * shard * pixels, transcendentals=0),
    )(own)
    outs = pl.pallas_call(
        functools.partial(pair_kernel, pix_count, rows, breadth, channels),
        out_shape=out_shapes,
        in_specs=[vmem] * (1 + count) + [anywhere] * (2 * LEVELS),
        out_specs=[anywhere] * (2 * LEVELS),
        scratch_shapes=[
            pltpu.VMEM((pixels, channels), jnp.bfloat16),
            pltpu.VMEM((channels // LANES, pixels // 2, LANES), jnp.float32),
            pltpu.VMEM((pixels // 4, channels), jnp.float32),
            pltpu.VMEM((pixels // 16, channels), jnp.float32),
        ]
        + staging
        + [pltpu.SemaphoreType.DMA((LEVELS,))],
        input_output_aliases={1 + count + i: i for i in range(2 * LEVELS)},
        compiler_params=limits,
        cost_estimate=pl.CostEstimate(flops=4 * shard * pixels * channels, bytes_accessed=4 * shard * pixels, transcendentals=0),
    )(near, *shards, *blanks)
    result = []
    for d in range(2):
        full, half, quarter, eighth = outs[d * LEVELS : (d + 1) * LEVELS]
        result += [full[None], half[None], jnp.transpose(quarter, (0, 2, 1))[None], jnp.transpose(eighth, (1, 2, 0))[None]]
    return tuple(result)


def per_device(frame_count, pix_count, features):
    rows, breadth, channels = features.shape[1:]
    fits = frame_count == 2 and pix_count & (pix_count - 1) == 0 and (rows * pix_count) % 8 == 0 and breadth % 32 == 0 and channels % LANES == 0
    return two_frames(features) if fits else many_frames(features)


def solution(mesh):
    spec = P(("clip", "frame"), "pix", None, None)

    def body(features):
        return per_device(mesh.shape["frame"], mesh.shape["pix"], features)

    return jax.shard_map(
        body, mesh=mesh, in_specs=(spec,), out_specs=(spec,) * (2 * LEVELS), check_vma=False
    )
```

profile of v0, /device:TPU:0, one launch (start us, length us, event | category | flops | bytes accessed | tf_op | source)
XLA Modules:
  0.0 16.7 jit_solution(13812280636963171240)
XLA Ops:
  0.6 5.0 %collective-permute-start = (bf16[192,256]{1,0:T(8,128)(2,1)}, bf16[192,256]{1,0:T(8,128)(2,1)S(1)}, u32[]{:S(2)}, u32[]{:S(2)}) collective-permute-start(bf16[192,256]{1,0:T(8,128)(2,1)} %bitcast.17), channel_id=1, source_target_pairs={{0,6},{1,4},{2,7},{3,5},{4,2},{5,0},{6,3},{7,1},{8,14},{9,12},{10,... | collective-permute-start | bytes 294920 | tf_op jit(solution)/shard_map/ppermute | solution.py:180
  5.7 0.5 %collective-permute-start.2 = (bf16[192,256]{1,0:T(8,128)(2,1)}, bf16[192,256]{1,0:T(8,128)(2,1)S(1)}, u32[]{:S(2)}, u32[]{:S(2)}) collective-permute-start(bf16[192,256]{1,0:T(8,128)(2,1)} %bitcast.18), channel_id=1, source_target_pairs={{0,4},{1,6},{2,5},{3,7},{4,0},{5,2},{6,1},{7,3},{8,12},{9,14},{10,... | collective-permute-start | bytes 294920 | tf_op jit(solution)/shard_map/ppermute | solution.py:180
  6.2 2.5 %collective-permute-start.1 = (bf16[192,256]{1,0:T(8,128)(2,1)}, bf16[192,256]{1,0:T(8,128)(2,1)S(1)}, u32[]{:S(2)}, u32[]{:S(2)}) collective-permute-start(bf16[192,256]{1,0:T(8,128)(2,1)} %bitcast.19), channel_id=1, source_target_pairs={{0,5},{1,7},{2,4},{3,6},{4,1},{5,3},{6,0},{7,2},{8,13},{9,15},{10,... | collective-permute-start | bytes 294920 | tf_op jit(solution)/shard_map/ppermute | solution.py:180
  8.7 0.0 collective-permute-done.refs_0_
  8.7 1.7 %collective-permute-start.3 = (bf16[192,256]{1,0:T(8,128)(2,1)S(1)}, bf16[192,256]{1,0:T(8,128)(2,1)S(1)}, u32[]{:S(2)}, u32[]{:S(2)}) collective-permute-start(bf16[192,256]{1,0:T(8,128)(2,1)S(1)} %collective-permute-done.refs_0_), channel_id=1, source_target_pairs={{0,1},{1,0},{2,3},{3,2},{4,5},{5,4},{6,7},{7,6},{8,9},{9,8},{10,11... | collective-permute-start | bytes 294920 | tf_op jit(solution)/shard_map/ppermute | solution.py:182
  10.4 0.0 copy-start
  10.4 0.9 %copy-done = bf16[1,2,96,256]{3,2,1,0:T(8,128)(2,1)S(1)} copy-done((bf16[1,2,96,256]{3,2,1,0:T(8,128)(2,1)S(1)}, bf16[1,2,96,256]{3,2,1,0:T(8,128)(2,1)}, u32[]{:S(2)}) %copy-start) | copy-done | bytes 98328
  11.3 0.9 %shard_map.78 = (bf16[192,256]{1,0:T(8,128)(2,1)S(1)}, bf16[2,96,768]{2,1,0:T(8,128)(2,1)}, bf16[2,96,192]{2,1,0:T(8,128)(2,1)}, bf16[2,48,96]{2,1,0:T(8,128)(2,...) custom-call(bf16[192,256]{1,0:T(8,128)(2,1)S(1)} %bitcast.20), custom_call_target="tpu_custom_call" | custom-call | flops 37748736 | bytes 589824 | tf_op jit(solution)/shard_map/pallas_call | solution.py:206
  12.2 0.0 collective-permute-done.2.refs_2_
  12.2 2.3 %collective-permute-done.1.refs_1_ = bf16[192,256]{1,0:T(8,128)(2,1)S(1)} collective-permute-done((bf16[192,256]{1,0:T(8,128)(2,1)}, bf16[192,256]{1,0:T(8,128)(2,1)S(1)}, u32[]{:S(2)}, u32[]{:S(2)}) %collective-permute-start.1) | collective-permute-done | bytes 98336 | tf_op jit(solution)/shard_map/ppermute | solution.py:180
  14.5 0.9 %collective-permute-done.3.refs_3_ = bf16[192,256]{1,0:T(8,128)(2,1)S(1)} collective-permute-done((bf16[192,256]{1,0:T(8,128)(2,1)S(1)}, bf16[192,256]{1,0:T(8,128)(2,1)S(1)}, u32[]{:S(2)}, u32[]{:S(2)}) %collective-permute-start.3) | collective-permute-done | bytes 98336 | tf_op jit(solution)/shard_map/ppermute | solution.py:182
  15.4 1.3 %shard_map.79 = (bf16[2,96,768]{2,1,0:T(8,128)(2,1)}, bf16[2,96,192]{2,1,0:T(8,128)(2,1)}, bf16[2,48,96]{2,1,0:T(8,128)(2,1)}, bf16[12,2,96]{2,1,0:T(2,128)(2,1)...) custom-call(bf16[192,256]{1,0:T(8,128)(2,1)S(1)} %get-tuple-element., ...), custom_call_target="tpu_custom_call", output_to_operand_aliasing={{0}: (5, {}), {1}: (6, {}), {2}: (7, {}), {3}: (8, {}), {4}... | custom-call | flops 150994944 | bytes 589824 | tf_op jit(solution)/shard_map/pallas_call | solution.py:215
Async XLA Ops:
  0.6 8.1 %collective-permute-start = (bf16[192,256]{1,0:T(8,128)(2,1)}, bf16[192,256]{1,0:T(8,128)(2,1)S(1)}, u32[]{:S(2)}, u32[]{:S(2)}) collective-permute-start(bf16[192,256]{1,0:T(8,128)(2,1)} %bitcast.17), channel_id=1, source_target_pairs={{0,6},{1,4},{2,7},{3,5},{4,2},{5,0},{6,3},{7,1},{8,14},{9,12},{10,... | collective-permute-start | bytes 294920 | tf_op jit(solution)/shard_map/ppermute | solution.py:180
  5.7 6.5 %collective-permute-start.2 = (bf16[192,256]{1,0:T(8,128)(2,1)}, bf16[192,256]{1,0:T(8,128)(2,1)S(1)}, u32[]{:S(2)}, u32[]{:S(2)}) collective-permute-start(bf16[192,256]{1,0:T(8,128)(2,1)} %bitcast.18), channel_id=1, source_target_pairs={{0,4},{1,6},{2,5},{3,7},{4,0},{5,2},{6,1},{7,3},{8,12},{9,14},{10,... | collective-permute-start | bytes 294920 | tf_op jit(solution)/shard_map/ppermute | solution.py:180
  6.2 8.3 %collective-permute-start.1 = (bf16[192,256]{1,0:T(8,128)(2,1)}, bf16[192,256]{1,0:T(8,128)(2,1)S(1)}, u32[]{:S(2)}, u32[]{:S(2)}) collective-permute-start(bf16[192,256]{1,0:T(8,128)(2,1)} %bitcast.19), channel_id=1, source_target_pairs={{0,5},{1,7},{2,4},{3,6},{4,1},{5,3},{6,0},{7,2},{8,13},{9,15},{10,... | collective-permute-start | bytes 294920 | tf_op jit(solution)/shard_map/ppermute | solution.py:180
  8.7 6.7 %collective-permute-start.3 = (bf16[192,256]{1,0:T(8,128)(2,1)S(1)}, bf16[192,256]{1,0:T(8,128)(2,1)S(1)}, u32[]{:S(2)}, u32[]{:S(2)}) collective-permute-start(bf16[192,256]{1,0:T(8,128)(2,1)S(1)} %collective-permute-done.refs_0_), channel_id=1, source_target_pairs={{0,1},{1,0},{2,3},{3,2},{4,5},{5,4},{6,7},{7,6},{8,9},{9,8},{10,11... | collective-permute-start | bytes 294920 | tf_op jit(solution)/shard_map/ppermute | solution.py:182
  10.4 0.9 %copy-start = (bf16[1,2,96,256]{3,2,1,0:T(8,128)(2,1)S(1)}, bf16[1,2,96,256]{3,2,1,0:T(8,128)(2,1)}, u32[]{:S(2)}) copy-start(bf16[1,2,96,256]{3,2,1,0:T(8,128)(2,1)} %param.1) | copy-start | bytes 294916
where the time goes:
time: 16.9 us; the launch traced here: 16.7 us
  starting transfers between devices  9.74 us (58%)
  waiting for transfers between devices  3.26 us (19%)
  Pallas kernels  2.19 us (13%)
  local copies, waits for them, and re-layouts  0.89 us (5%)
  between operations  0.65 us (4%)
    ppermute x3, starting transfers between devices, exchange(): got.append(lax.ppermute(own, ('frame', 'pix'), pairs))  8.08 us
    ppermute x3, waiting for transfers between devices, exchange(): got.append(lax.ppermute(own, ('frame', 'pix'), pairs))  2.31 us
    ppermute x1, starting transfers between devices, exchange(): lax.ppermute(got[0], 'pix', [(p, p ^ 1) for p in range(pix_count)])  1.66 us
    pallas_call x1, Pallas kernels, two_frames(): pl.pallas_call(functools.partial(pair_kernel, pix_count, rows, breadth, c...  1.3 us
    ppermute x1, waiting for transfers between devices, exchange(): lax.ppermute(got[0], 'pix', [(p, p ^ 1) for p in range(pix_count)])  0.95 us
    pallas_call x1, Pallas kernels, two_frames(): pl.pallas_call(blank_kernel, out_shape=[jax.ShapeDtypeStruct(own.shape, o...  0.9 us
    unnamed x2, local copies, waits for them, and re-layouts  0.89 us
  transfers between devices with their start and end apart: 4, of which 2 were waited for; matrix products, arithmetic and copies ran while one was open for 0% of the time, Pallas kernels for 5%

commit v1 on v0

v1 whole, which is shorter than its diff:
```python
import functools
import math

import jax
import jax.numpy as jnp
from jax import lax
from jax.experimental import pallas as pl
from jax.experimental.pallas import tpu as pltpu
from jax.sharding import PartitionSpec as P


LEVELS = 4
LANES = 128


def from_behind(value, axis, steps):
    count = lax.axis_size(axis)
    leading, last = (max(0, -steps), min(count, count - steps))
    return lax.ppermute(value, axis, [(source, source + steps) for source in range(leading, last)])


def halved(current):
    count, height, breadth = current.shape
    return current.reshape(count, height // 2, 2, breadth // 2, 2).mean(axis=(2, 4))


def pyramid_of(scores, row_count, breadth):
    height = scores.shape[1] // breadth
    current = scores.reshape(scores.shape[0], height, breadth)
    result = []
    for depth_index in range(LEVELS):
        result.append(current.reshape(1, row_count, breadth, -1).astype(jnp.bfloat16))
        if depth_index < LEVELS - 1:
            current = halved(current)
    return result


def many_frames(features):
    row_count, breadth, channels = features.shape[1:]
    own_pixels = features.reshape(row_count * breadth, channels)
    factor = 1.0 / math.sqrt(channels)
    result = []
    for steps in (-1, 1):
        neighbour = from_behind(own_pixels, "frame", steps)
        target = lax.all_gather(neighbour, "pix", axis=0, tiled=True)
        product = lax.dot_general(
            own_pixels, target, (((1,), (1,)), ((), ())), preferred_element_type=jnp.float32
        )
        result += pyramid_of(product * factor, row_count, breadth)
    return tuple(result)


def dot_nt(left, right):
    return lax.dot_general(left, right, (((1,), (1,)), ((), ())), preferred_element_type=jnp.float32)


def by_frame(first, second):
    frame = lax.axis_index("frame")
    pl.when(frame == 0)(first)
    pl.when(frame != 0)(second)


def send(level, piece, source, forward, backward, sems, columns=None):
    def start(targets):
        target = targets[level] if columns is None else targets[level].at[:, :, columns]
        return lambda: pltpu.make_async_copy(source, target, sems.at[piece]).start()

    by_frame(start(forward), start(backward))


def blank_kernel(features_ref, own_ref, *refs):
    outs, (*blanks, sems, own_sem) = refs[: 2 * LEVELS], refs[2 * LEVELS :]
    forward, backward = outs[:LEVELS], outs[LEVELS:]
    fetch = pltpu.make_async_copy(features_ref, own_ref, own_sem)
    fetch.start()
    for level, blank in enumerate(blanks):
        blank[...] = jnp.zeros_like(blank)
        send(level, level, blank, backward, forward, sems)
    for level, blank in enumerate(blanks):
        pltpu.make_async_copy(blank, backward[level], sems.at[level]).wait()
    fetch.wait()


def place_of(origin):
    pix = lax.axis_index("pix")
    return sum(jnp.where(pix == q, p, 0) for q, p in enumerate(origin))


def paired(line, summed, breadth):
    parts = []
    for c in range(line.shape[1] // LANES):
        summed[c, :breadth, :] = line[:, c * LANES : (c + 1) * LANES]
    for c in range(line.shape[1] // LANES):
        even = summed[c, pl.ds(0, breadth // 2, stride=2), :]
        odd = summed[c, pl.ds(1, breadth // 2, stride=2), :]
        parts.append((even + odd) * 0.25)
    return jnp.concatenate(parts, axis=1)


def level1_of(shard_ref, summed, breadth):
    upper = shard_ref[:breadth, :].astype(jnp.float32)
    return paired(upper + shard_ref[breadth : 2 * breadth, :].astype(jnp.float32), summed, breadth)


def split(value):
    high = value.astype(jnp.bfloat16)
    return high, (value - high.astype(jnp.float32)).astype(jnp.bfloat16)


def early_kernel(pix_count, breadth, own_ref, *refs):
    origins = origins_of(pix_count)
    count = len(origins) - 1
    shards, (scores_ref, partner_ref, high_ref, low_ref, partner1_ref, level2_ref) = refs[:count], refs[count : count + 6]
    target, level1, *summed = refs[count + 6 :]
    shard = own_ref.shape[0]
    half = breadth // 2
    last = place_of(origins[-1])
    far = 1 - last // 2
    factor = 1.0 / math.sqrt(own_ref.shape[1])
    for i, ref in enumerate(shards):
        place = place_of(origins[i])
        target[pl.ds(pl.multiple_of(place * shard, shard), shard), :] = ref[...]
        means = level1_of(ref, summed[i], breadth)
        at = pl.ds(pl.multiple_of(place * half, half), half)
        level1[at, :] = means
        high_ref[at, :], low_ref[at, :] = split(means)
    pair = target[pl.ds(pl.multiple_of(far * 2 * shard, 2 * shard), 2 * shard), :]
    scores = (dot_nt(own_ref[...], pair) * factor).astype(scores_ref.dtype)
    for r in range(2):
        scores_ref[r] = scores[r * breadth : (r + 1) * breadth, :]
    partner = last + 1 - 2 * (last % 2)
    partner_ref[...] = target[pl.ds(pl.multiple_of(partner * shard, shard), shard), :]
    partner1_ref[...] = level1[pl.ds(pl.multiple_of(partner * half, half), half), :]
    upper = level1[pl.ds(pl.multiple_of(far * breadth, half), half), :]
    lower = level1[pl.ds(pl.multiple_of(far * breadth + half, half), half), :]
    level2_ref[...] = paired(upper + lower, summed[0], half)


def late_kernel(pix_count, breadth, *refs):
    own_ref, relayed_ref, scores_ref, partner_ref, high_ref, low_ref, partner1_ref, far2_ref = refs[:8]
    outs, (target, highs, lows, level2, level3, summed, near_scores, v1, v2, v3, sems) = refs[8 + 2 * LEVELS : 8 + 4 * LEVELS], refs[8 + 4 * LEVELS :]
    forward, backward = outs[:LEVELS], outs[LEVELS:]
    shard = own_ref.shape[0]
    half, quarter = breadth // 2, breadth // 4
    last = place_of(origins_of(pix_count)[-1])
    near = last // 2
    far = 1 - near
    factor = 1.0 / math.sqrt(own_ref.shape[1])

    def columns(pair):
        return pl.ds(pl.multiple_of(pair * 2 * shard, 2 * shard), 2 * shard)

    send(0, LEVELS, scores_ref, forward, backward, sems, columns(far))
    odd = last % 2
    target[pl.ds(pl.multiple_of(odd * shard, shard), shard), :] = relayed_ref[...]
    target[pl.ds(pl.multiple_of((1 - odd) * shard, shard), shard), :] = partner_ref[...]
    level1 = level1_of(relayed_ref, summed, breadth)
    highs[...] = high_ref[...]
    lows[...] = low_ref[...]
    at = pl.ds(pl.multiple_of(last * half, half), half)
    highs[at, :], lows[at, :] = split(level1)
    level2[pl.ds(pl.multiple_of(near * quarter, quarter), quarter), :] = paired(level1 + partner1_ref[...], summed, half)
    level2[pl.ds(pl.multiple_of(far * quarter, quarter), quarter), :] = far2_ref[...]
    eighth = quarter // 2
    level3[...] = jnp.zeros_like(level3)
    level3[:eighth, :] = paired(level2[:quarter, :] + level2[quarter:, :], summed, quarter)
    own = own_ref[...]
    scores = (dot_nt(own, target[...]) * factor).astype(near_scores.dtype)
    halves = ((dot_nt(own, highs[...]) + dot_nt(own, lows[...])) * factor).astype(v1.dtype)
    coarse = jnp.concatenate([*split(level2[...]), *split(level3[...])], axis=0)
    lines = []
    for r in range(2):
        near_scores[r] = scores[r * breadth : (r + 1) * breadth, :]
        v1[r] = halves[r * breadth : (r + 1) * breadth, :]
        product = dot_nt(coarse, own[r * breadth : (r + 1) * breadth, :]) * factor
        v2[r] = (product[:half, :] + product[half:breadth, :]).astype(v2.dtype)
        product = product[breadth:, :]
        lines.append(product[:eighth, :] + product[level3.shape[0] : level3.shape[0] + eighth, :])
    v3[...] = jnp.stack(lines, axis=1).astype(v3.dtype)
    pieces = ((0, 0, near_scores, columns(near)), (1, 1, v1, None), (2, 2, v2, None), (3, 3, v3, None))

    def start(targets):
        def run():
            for level, piece, source, where in pieces:
                target = targets[level] if where is None else targets[level].at[:, :, where]
                pltpu.make_async_copy(source, target, sems.at[piece]).start()

        return run

    by_frame(start(forward), start(backward))
    pltpu.make_async_copy(scores_ref, forward[0].at[:, :, columns(far)], sems.at[LEVELS]).wait()
    pltpu.make_async_copy(near_scores, forward[0].at[:, :, columns(near)], sems.at[0]).wait()
    for level, value in ((1, v1), (2, v2), (3, v3)):
        pltpu.make_async_copy(value, forward[level], sems.at[level]).wait()


ROUNDS = ((2, 0, 3, 1), (1, 3, 0, 2), (0, 2, 1, 3))


def origins_of(pix_count):
    origins = [[row.index(q) for q in range(pix_count)] for row in ROUNDS]
    return origins + [[ROUNDS[0].index(q ^ 1) for q in range(pix_count)]]


def exchange(own, pix_count):
    got = []
    for row in ROUNDS:
        pairs = [(f * pix_count + p, (1 - f) * pix_count + row[p]) for f in range(2) for p in range(pix_count)]
        got.append(lax.ppermute(own, ("frame", "pix"), pairs))
    got.append(lax.ppermute(got[0], "pix", [(p, p ^ 1) for p in range(pix_count)]))
    return got


def two_frames(features):
    rows, breadth, channels = features.shape[1:]
    pix_count = lax.axis_size("pix")
    shard = rows * breadth
    pixels = shard * pix_count
    own = features.reshape(shard, channels)
    *direct, relayed = exchange(own, pix_count)

    shapes = [
        (rows, breadth, pixels),
        (rows, breadth, pixels // 4),
        (rows, pixels // 16, breadth),
        (pixels // 64, rows, breadth),
    ]
    vmem = pl.BlockSpec(memory_space=pltpu.VMEM)
    anywhere = pl.BlockSpec(memory_space=pl.ANY)
    hbm = pl.BlockSpec(memory_space=pltpu.HBM)
    out_shapes = [jax.ShapeDtypeStruct(s, jnp.bfloat16) for s in shapes * 2]
    limits = pltpu.CompilerParams(vmem_limit_bytes=12 * 2**20)

    def cost(flops):
        return pl.CostEstimate(flops=flops, bytes_accessed=4 * shard * pixels, transcendentals=0)

    def scratch(kind, *shape):
        return pltpu.VMEM(shape, kind)

    flops = shard * pixels * channels
    near, *blanks = pl.pallas_call(
        blank_kernel,
        out_shape=[jax.ShapeDtypeStruct(own.shape, own.dtype)] + out_shapes,
        in_specs=[hbm],
        out_specs=[vmem] + [anywhere] * (2 * LEVELS),
        scratch_shapes=[scratch(jnp.bfloat16, *s) for s in shapes]
        + [pltpu.SemaphoreType.DMA((LEVELS,)), pltpu.SemaphoreType.DMA],
        compiler_params=limits,
        cost_estimate=cost(flops),
    )(own)
    early = pl.pallas_call(
        functools.partial(early_kernel, pix_count, breadth),
        out_shape=[
            jax.ShapeDtypeStruct((rows, breadth, 2 * shard), jnp.bfloat16),
            jax.ShapeDtypeStruct((shard, channels), jnp.bfloat16),
            jax.ShapeDtypeStruct((pixels // 4, channels), jnp.bfloat16),
            jax.ShapeDtypeStruct((pixels // 4, channels), jnp.bfloat16),
            jax.ShapeDtypeStruct((shard // 4, channels), jnp.float32),
            jax.ShapeDtypeStruct((shard // 8, channels), jnp.float32),
        ],
        in_specs=[vmem] * (1 + len(direct)),
        out_specs=[vmem] * 6,
        scratch_shapes=[
            scratch(jnp.bfloat16, pixels, channels),
            scratch(jnp.float32, pixels // 4, channels),
        ]
        + [scratch(jnp.float32, channels // LANES, breadth, LANES)] * len(direct),
        compiler_params=limits,
        cost_estimate=cost(2 * flops),
    )(near, *direct)
    outs = pl.pallas_call(
        functools.partial(late_kernel, pix_count, breadth),
        out_shape=out_shapes,
        in_specs=[vmem] * 8 + [anywhere] * (2 * LEVELS),
        out_specs=[anywhere] * (2 * LEVELS),
        scratch_shapes=[
            scratch(jnp.bfloat16, 2 * shard, channels),
            scratch(jnp.bfloat16, pixels // 4, channels),
            scratch(jnp.bfloat16, pixels // 4, channels),
            scratch(jnp.float32, pixels // 16, channels),
            scratch(jnp.float32, -(-pixels // 64 // 16) * 16, channels),
            scratch(jnp.float32, channels // LANES, breadth, LANES),
            scratch(jnp.bfloat16, rows, breadth, 2 * shard),
        ]
        + [scratch(jnp.bfloat16, *s) for s in shapes[1:]]
        + [pltpu.SemaphoreType.DMA((LEVELS + 1,))],
        input_output_aliases={8 + i: i for i in range(2 * LEVELS)},
        compiler_params=limits,
        cost_estimate=cost(2 * flops),
    )(near, relayed, *early, *blanks)
    result = []
    for d in range(2):
        full, half, quarter, eighth = outs[d * LEVELS : (d + 1) * LEVELS]
        result += [full[None], half[None], jnp.transpose(quarter, (0, 2, 1))[None], jnp.transpose(eighth, (1, 2, 0))[None]]
    return tuple(result)


def per_device(frame_count, pix_count, features):
    rows, breadth, channels = features.shape[1:]
    fits = frame_count == 2 and pix_count == len(ROUNDS) + 1 and rows == 2 and breadth % 32 == 0 and channels % LANES == 0
    return two_frames(features) if fits and 2 * rows * breadth % LANES == 0 else many_frames(features)


def solution(mesh):
    spec = P(("clip", "frame"), "pix", None, None)

    def body(features):
        return per_device(mesh.shape["frame"], mesh.shape["pix"], features)

    return jax.shard_map(
        body, mesh=mesh, in_specs=(spec,), out_specs=(spec,) * (2 * LEVELS), check_vma=False
    )
```

time: 16.9 us -> 16.6 us (0.982)
  waiting for transfers between devices: 3.26 us -> 2.92 us
    ppermute x1, waiting for transfers between devices: 0.95 us -> 0.62 us  [exchange(): lax.ppermute(got[0], 'pix', [(p, p ^ 1) for p in range(pix_count)])]
    pallas_call x1 -> x2, Pallas kernels: 1.3 us -> 1.37 us  [the longest x1 1.04 us: two_frames(): pl.pallas_call(functools.partial(late_kernel, pix_count, breadth), out_sh...]
  transfers between devices with their start and end apart: 4 -> 4, of which waited for: 2 -> 2; matrix products, arithmetic and copies ran while one was open for 0% -> 0% of each run, Pallas kernels for 5% -> 7%
where the time goes in v1:
time: 16.6 us; the launch traced here: 16.5 us
  starting transfers between devices  9.74 us (59%)
  waiting for transfers between devices  2.92 us (18%)
  Pallas kernels  2.26 us (14%)
  local copies, waits for them, and re-layouts  0.89 us (5%)
  between operations  0.66 us (4%)
    ppermute x3, starting transfers between devices, exchange(): got.append(lax.ppermute(own, ('frame', 'pix'), pairs))  8.08 us
    ppermute x3, waiting for transfers between devices, exchange(): got.append(lax.ppermute(own, ('frame', 'pix'), pairs))  2.31 us
    ppermute x1, starting transfers between devices, exchange(): lax.ppermute(got[0], 'pix', [(p, p ^ 1) for p in range(pix_count)])  1.66 us
    pallas_call x1, Pallas kernels, two_frames(): pl.pallas_call(functools.partial(late_kernel, pix_count, breadth), out_sh...  1.04 us
    pallas_call x1, Pallas kernels, two_frames(): pl.pallas_call(blank_kernel, out_shape=[jax.ShapeDtypeStruct(own.shape, o...  0.9 us
    unnamed x2, local copies, waits for them, and re-layouts  0.89 us
    ppermute x1, waiting for transfers between devices, exchange(): lax.ppermute(got[0], 'pix', [(p, p ^ 1) for p in range(pix_count)])  0.62 us
  transfers between devices with their start and end apart: 4, of which 2 were waited for; matrix products, arithmetic and copies ran while one was open for 0% of the time, Pallas kernels for 7%

profile of v1, /device:TPU:0, one launch (start us, length us, event | category | flops | bytes accessed | tf_op | source)
XLA Modules:
  0.0 16.5 jit_solution(5799106781841713971)
XLA Ops:
  0.6 5.0 %collective-permute-start = (bf16[192,256]{1,0:T(8,128)(2,1)}, bf16[192,256]{1,0:T(8,128)(2,1)S(1)}, u32[]{:S(2)}, u32[]{:S(2)}) collective-permute-start(bf16[192,256]{1,0:T(8,128)(2,1)} %bitcast.17), channel_id=1, source_target_pairs={{0,6},{1,4},{2,7},{3,5},{4,2},{5,0},{6,3},{7,1},{8,14},{9,12},{10,... | collective-permute-start | bytes 294920 | tf_op jit(solution)/shard_map/ppermute | solution.py:209
  5.7 0.5 %collective-permute-start.3 = (bf16[192,256]{1,0:T(8,128)(2,1)}, bf16[192,256]{1,0:T(8,128)(2,1)S(1)}, u32[]{:S(2)}, u32[]{:S(2)}) collective-permute-start(bf16[192,256]{1,0:T(8,128)(2,1)} %bitcast.18), channel_id=1, source_target_pairs={{0,4},{1,6},{2,5},{3,7},{4,0},{5,2},{6,1},{7,3},{8,12},{9,14},{10,... | collective-permute-start | bytes 294920 | tf_op jit(solution)/shard_map/ppermute | solution.py:209
  6.2 2.5 %collective-permute-start.2 = (bf16[192,256]{1,0:T(8,128)(2,1)}, bf16[192,256]{1,0:T(8,128)(2,1)S(1)}, u32[]{:S(2)}, u32[]{:S(2)}) collective-permute-start(bf16[192,256]{1,0:T(8,128)(2,1)} %bitcast.19), channel_id=1, source_target_pairs={{0,5},{1,7},{2,4},{3,6},{4,1},{5,3},{6,0},{7,2},{8,13},{9,15},{10,... | collective-permute-start | bytes 294920 | tf_op jit(solution)/shard_map/ppermute | solution.py:209
  8.7 0.0 collective-permute-done.refs_0_
  8.7 1.7 %collective-permute-start.1 = (bf16[192,256]{1,0:T(8,128)(2,1)S(1)}, bf16[192,256]{1,0:T(8,128)(2,1)S(1)}, u32[]{:S(2)}, u32[]{:S(2)}) collective-permute-start(bf16[192,256]{1,0:T(8,128)(2,1)S(1)} %collective-permute-done.refs_0_), channel_id=1, source_target_pairs={{0,1},{1,0},{2,3},{3,2},{4,5},{5,4},{6,7},{7,6},{8,9},{9,8},{10,11... | collective-permute-start | bytes 294920 | tf_op jit(solution)/shard_map/ppermute | solution.py:210
  10.4 0.0 copy-start
  10.4 0.9 %copy-done = bf16[1,2,96,256]{3,2,1,0:T(8,128)(2,1)S(1)} copy-done((bf16[1,2,96,256]{3,2,1,0:T(8,128)(2,1)S(1)}, bf16[1,2,96,256]{3,2,1,0:T(8,128)(2,1)}, u32[]{:S(2)}) %copy-start) | copy-done | bytes 98328
  11.3 0.9 %shard_map.78 = (bf16[192,256]{1,0:T(8,128)(2,1)S(1)}, bf16[2,96,768]{2,1,0:T(8,128)(2,1)}, bf16[2,96,192]{2,1,0:T(8,128)(2,1)}, bf16[2,48,96]{2,1,0:T(8,128)(2,...) custom-call(bf16[192,256]{1,0:T(8,128)(2,1)S(1)} %bitcast.20), custom_call_target="tpu_custom_call" | custom-call | flops 37748736 | bytes 589824 | tf_op jit(solution)/shard_map/pallas_call | solution.py:241
  12.2 0.0 collective-permute-done.3.refs_2_
  12.2 2.3 %collective-permute-done.2.refs_1_ = bf16[192,256]{1,0:T(8,128)(2,1)S(1)} collective-permute-done((bf16[192,256]{1,0:T(8,128)(2,1)}, bf16[192,256]{1,0:T(8,128)(2,1)S(1)}, u32[]{:S(2)}, u32[]{:S(2)}) %collective-permute-start.2) | collective-permute-done | bytes 98336 | tf_op jit(solution)/shard_map/ppermute | solution.py:209
  14.5 0.3 %shard_map.79 = (bf16[2,96,384]{2,1,0:T(8,128)(2,1)S(1)}, bf16[192,256]{1,0:T(8,128)(2,1)S(1)}, bf16[192,256]{1,0:T(8,128)(2,1)S(1)}, bf16[192,256]{1,0:T(8,128)...) custom-call(bf16[192,256]{1,0:T(8,128)(2,1)S(1)} %get-tuple-element.31.own_ref.refs_0_, ...), custom_call_target="tpu_custom_call" | custom-call | flops 75497472 | bytes 589824 | tf_op jit(solution)/shard_map/pallas_call | solution.py:251
  14.8 0.6 %collective-permute-done.1.refs_1_ = bf16[192,256]{1,0:T(8,128)(2,1)S(1)} collective-permute-done((bf16[192,256]{1,0:T(8,128)(2,1)S(1)}, bf16[192,256]{1,0:T(8,128)(2,1)S(1)}, u32[]{:S(2)}, u32[]{:S(2)}) %collective-permute-start.1) | collective-permute-done | bytes 98336 | tf_op jit(solution)/shard_map/ppermute | solution.py:210
  15.4 1.0 %shard_map.80 = (bf16[2,96,768]{2,1,0:T(8,128)(2,1)}, bf16[2,96,192]{2,1,0:T(8,128)(2,1)}, bf16[2,48,96]{2,1,0:T(8,128)(2,1)}, bf16[12,2,96]{2,1,0:T(2,128)(2,1)...) custom-call(bf16[192,256]{1,0:T(8,128)(2,1)S(1)} %get-tuple-element., ...), custom_call_target="tpu_custom_call", output_to_operand_aliasing={{0}: (8, {}), {1}: (9, {}), {2}: (10, {}), {3}: (11, {}), {... | custom-call | flops 75497472 | bytes 589824 | tf_op jit(solution)/shard_map/pallas_call | solution.py:271
Async XLA Ops:
  0.6 8.1 %collective-permute-start = (bf16[192,256]{1,0:T(8,128)(2,1)}, bf16[192,256]{1,0:T(8,128)(2,1)S(1)}, u32[]{:S(2)}, u32[]{:S(2)}) collective-permute-start(bf16[192,256]{1,0:T(8,128)(2,1)} %bitcast.17), channel_id=1, source_target_pairs={{0,6},{1,4},{2,7},{3,5},{4,2},{5,0},{6,3},{7,1},{8,14},{9,12},{10,... | collective-permute-start | bytes 294920 | tf_op jit(solution)/shard_map/ppermute | solution.py:209
  5.7 6.5 %collective-permute-start.3 = (bf16[192,256]{1,0:T(8,128)(2,1)}, bf16[192,256]{1,0:T(8,128)(2,1)S(1)}, u32[]{:S(2)}, u32[]{:S(2)}) collective-permute-start(bf16[192,256]{1,0:T(8,128)(2,1)} %bitcast.18), channel_id=1, source_target_pairs={{0,4},{1,6},{2,5},{3,7},{4,0},{5,2},{6,1},{7,3},{8,12},{9,14},{10,... | collective-permute-start | bytes 294920 | tf_op jit(solution)/shard_map/ppermute | solution.py:209
  6.2 8.3 %collective-permute-start.2 = (bf16[192,256]{1,0:T(8,128)(2,1)}, bf16[192,256]{1,0:T(8,128)(2,1)S(1)}, u32[]{:S(2)}, u32[]{:S(2)}) collective-permute-start(bf16[192,256]{1,0:T(8,128)(2,1)} %bitcast.19), channel_id=1, source_target_pairs={{0,5},{1,7},{2,4},{3,6},{4,1},{5,3},{6,0},{7,2},{8,13},{9,15},{10,... | collective-permute-start | bytes 294920 | tf_op jit(solution)/shard_map/ppermute | solution.py:209
  8.7 6.7 %collective-permute-start.1 = (bf16[192,256]{1,0:T(8,128)(2,1)S(1)}, bf16[192,256]{1,0:T(8,128)(2,1)S(1)}, u32[]{:S(2)}, u32[]{:S(2)}) collective-permute-start(bf16[192,256]{1,0:T(8,128)(2,1)S(1)} %collective-permute-done.refs_0_), channel_id=1, source_target_pairs={{0,1},{1,0},{2,3},{3,2},{4,5},{5,4},{6,7},{7,6},{8,9},{9,8},{10,11... | collective-permute-start | bytes 294920 | tf_op jit(solution)/shard_map/ppermute | solution.py:210
  10.4 0.9 %copy-start = (bf16[1,2,96,256]{3,2,1,0:T(8,128)(2,1)S(1)}, bf16[1,2,96,256]{3,2,1,0:T(8,128)(2,1)}, u32[]{:S(2)}) copy-start(bf16[1,2,96,256]{3,2,1,0:T(8,128)(2,1)} %param.1) | copy-start | bytes 294916

commit v2 on v1

--- a/solution.py
+++ b/solution.py
@@ -86,20 +86,21 @@
     return sum(jnp.where(pix == q, p, 0) for q, p in enumerate(origin))
 
 
-def paired(line, summed, breadth):
+def pooled(line, summed, step):
+    breadth = line.shape[0]
     parts = []
     for c in range(line.shape[1] // LANES):
-        summed[c, :breadth, :] = line[:, c * LANES : (c + 1) * LANES]
+        summed[c] = line[:, c * LANES : (c + 1) * LANES]
     for c in range(line.shape[1] // LANES):
-        even = summed[c, pl.ds(0, breadth // 2, stride=2), :]
-        odd = summed[c, pl.ds(1, breadth // 2, stride=2), :]
-        parts.append((even + odd) * 0.25)
+        total = summed[c, pl.ds(0, breadth // step, stride=step), :]
+        for i in range(1, step):
+            total = total + summed[c, pl.ds(i, breadth // step, stride=step), :]
+        parts.append(total * (1.0 / (step * step)))
     return jnp.concatenate(parts, axis=1)
 
 
-def level1_of(shard_ref, summed, breadth):
-    upper = shard_ref[:breadth, :].astype(jnp.float32)
-    return paired(upper + shard_ref[breadth : 2 * breadth, :].astype(jnp.float32), summed, breadth)
+def line_of(shard_ref, breadth):
+    return shard_ref[:breadth, :].astype(jnp.float32) + shard_ref[breadth : 2 * breadth, :].astype(jnp.float32)
 
 
 def split(value):
@@ -110,8 +111,8 @@
 def early_kernel(pix_count, breadth, own_ref, *refs):
     origins = origins_of(pix_count)
     count = len(origins) - 1
-    shards, (scores_ref, partner_ref, high_ref, low_ref, partner1_ref, level2_ref) = refs[:count], refs[count : count + 6]
-    target, level1, *summed = refs[count + 6 :]
+    shards, (scores_ref, partner_ref, high_ref, low_ref, partner_line_ref, far_line_ref, far2_ref) = refs[:count], refs[count : count + 7]
+    target, lines, *summed = refs[count + 7 :]
     shard = own_ref.shape[0]
     half = breadth // 2
     last = place_of(origins[-1])
@@ -120,25 +121,26 @@
     for i, ref in enumerate(shards):
         place = place_of(origins[i])
         target[pl.ds(pl.multiple_of(place * shard, shard), shard), :] = ref[...]
-        means = level1_of(ref, summed[i], breadth)
+        line = line_of(ref, breadth)
+        lines[pl.ds(pl.multiple_of(place * breadth, breadth), breadth), :] = line
         at = pl.ds(pl.multiple_of(place * half, half), half)
-        level1[at, :] = means
-        high_ref[at, :], low_ref[at, :] = split(means)
+        high_ref[at, :], low_ref[at, :] = split(pooled(line, summed[i], 2))
     pair = target[pl.ds(pl.multiple_of(far * 2 * shard, 2 * shard), 2 * shard), :]
     scores = (dot_nt(own_ref[...], pair) * factor).astype(scores_ref.dtype)
     for r in range(2):
         scores_ref[r] = scores[r * breadth : (r + 1) * breadth, :]
     partner = last + 1 - 2 * (last % 2)
     partner_ref[...] = target[pl.ds(pl.multiple_of(partner * shard, shard), shard), :]
-    partner1_ref[...] = level1[pl.ds(pl.multiple_of(partner * half, half), half), :]
-    upper = level1[pl.ds(pl.multiple_of(far * breadth, half), half), :]
-    lower = level1[pl.ds(pl.multiple_of(far * breadth + half, half), half), :]
-    level2_ref[...] = paired(upper + lower, summed[0], half)
+    partner_line_ref[...] = lines[pl.ds(pl.multiple_of(partner * breadth, breadth), breadth), :]
+    upper = lines[pl.ds(pl.multiple_of(far * 2 * breadth, breadth), breadth), :]
+    far_line = upper + lines[pl.ds(pl.multiple_of((far * 2 + 1) * breadth, breadth), breadth), :]
+    far_line_ref[...] = far_line
+    far2_ref[...] = pooled(far_line, summed[0], 4)
 
 
 def late_kernel(pix_count, breadth, *refs):
-    own_ref, relayed_ref, scores_ref, partner_ref, high_ref, low_ref, partner1_ref, far2_ref = refs[:8]
-    outs, (target, highs, lows, level2, level3, summed, near_scores, v1, v2, v3, sems) = refs[8 + 2 * LEVELS : 8 + 4 * LEVELS], refs[8 + 4 * LEVELS :]
+    own_ref, relayed_ref, scores_ref, partner_ref, high_ref, low_ref, partner_line_ref, far_line_ref, far2_ref = refs[:9]
+    outs, (target, highs, lows, level2, level3, sum1, sum2, sum3, near_scores, v1, v2, v3, sems) = refs[9 + 2 * LEVELS : 9 + 4 * LEVELS], refs[9 + 4 * LEVELS :]
     forward, backward = outs[:LEVELS], outs[LEVELS:]
     shard = own_ref.shape[0]
     half, quarter = breadth // 2, breadth // 4
@@ -154,16 +156,17 @@
     odd = last % 2
     target[pl.ds(pl.multiple_of(odd * shard, shard), shard), :] = relayed_ref[...]
     target[pl.ds(pl.multiple_of((1 - odd) * shard, shard), shard), :] = partner_ref[...]
-    level1 = level1_of(relayed_ref, summed, breadth)
+    line = line_of(relayed_ref, breadth)
+    near_line = line + partner_line_ref[...]
     highs[...] = high_ref[...]
     lows[...] = low_ref[...]
     at = pl.ds(pl.multiple_of(last * half, half), half)
-    highs[at, :], lows[at, :] = split(level1)
-    level2[pl.ds(pl.multiple_of(near * quarter, quarter), quarter), :] = paired(level1 + partner1_ref[...], summed, half)
+    highs[at, :], lows[at, :] = split(pooled(line, sum1, 2))
+    level2[pl.ds(pl.multiple_of(near * quarter, quarter), quarter), :] = pooled(near_line, sum2, 4)
     level2[pl.ds(pl.multiple_of(far * quarter, quarter), quarter), :] = far2_ref[...]
     eighth = quarter // 2
     level3[...] = jnp.zeros_like(level3)
-    level3[:eighth, :] = paired(level2[:quarter, :] + level2[quarter:, :], summed, quarter)
+    level3[:eighth, :] = pooled(near_line + far_line_ref[...], sum3, 8)
     own = own_ref[...]
     scores = (dot_nt(own, target[...]) * factor).astype(near_scores.dtype)
     halves = ((dot_nt(own, highs[...]) + dot_nt(own, lows[...])) * factor).astype(v1.dtype)
@@ -255,14 +258,15 @@
             jax.ShapeDtypeStruct((shard, channels), jnp.bfloat16),
             jax.ShapeDtypeStruct((pixels // 4, channels), jnp.bfloat16),
             jax.ShapeDtypeStruct((pixels // 4, channels), jnp.bfloat16),
-            jax.ShapeDtypeStruct((shard // 4, channels), jnp.float32),
+            jax.ShapeDtypeStruct((breadth, channels), jnp.float32),
+            jax.ShapeDtypeStruct((breadth, channels), jnp.float32),
             jax.ShapeDtypeStruct((shard // 8, channels), jnp.float32),
         ],
         in_specs=[vmem] * (1 + len(direct)),
-        out_specs=[vmem] * 6,
+        out_specs=[vmem] * 7,
         scratch_shapes=[
             scratch(jnp.bfloat16, pixels, channels),
-            scratch(jnp.float32, pixels // 4, channels),
+            scratch(jnp.float32, pix_count * breadth, channels),
         ]
         + [scratch(jnp.float32, channels // LANES, breadth, LANES)] * len(direct),
         compiler_params=limits,
@@ -271,7 +275,7 @@
     outs = pl.pallas_call(
         functools.partial(late_kernel, pix_count, breadth),
         out_shape=out_shapes,
-        in_specs=[vmem] * 8 + [anywhere] * (2 * LEVELS),
+        in_specs=[vmem] * 9 + [anywhere] * (2 * LEVELS),
         out_specs=[anywhere] * (2 * LEVELS),
         scratch_shapes=[
             scratch(jnp.bfloat16, 2 * shard, channels),
@@ -280,11 +284,13 @@
             scratch(jnp.float32, pixels // 16, channels),
             scratch(jnp.float32, -(-pixels // 64 // 16) * 16, channels),
             scratch(jnp.float32, channels // LANES, breadth, LANES),
+            scratch(jnp.float32, channels // LANES, breadth, LANES),
+            scratch(jnp.float32, channels // LANES, breadth, LANES),
             scratch(jnp.bfloat16, rows, breadth, 2 * shard),
         ]
         + [scratch(jnp.bfloat16, *s) for s in shapes[1:]]
         + [pltpu.SemaphoreType.DMA((LEVELS + 1,))],
-        input_output_aliases={8 + i: i for i in range(2 * LEVELS)},
+        input_output_aliases={9 + i: i for i in range(2 * LEVELS)},
         compiler_params=limits,
         cost_estimate=cost(2 * flops),
     )(near, relayed, *early, *blanks)

time: 16.6 us -> 16.6 us (level)
  transfers between devices with their start and end apart: 4 -> 4, of which waited for: 2 -> 2; matrix products, arithmetic and copies ran while one was open for 0% -> 0% of each run, Pallas kernels for 7% -> 8%
where the time goes in v2:
time: 16.6 us; the launch traced here: 16.5 us
  starting transfers between devices  9.74 us (59%)
  waiting for transfers between devices  2.89 us (17%)
  Pallas kernels  2.31 us (14%)
  local copies, waits for them, and re-layouts  0.89 us (5%)
  between operations  0.66 us (4%)
    ppermute x3, starting transfers between devices, exchange(): got.append(lax.ppermute(own, ('frame', 'pix'), pairs))  8.08 us
    ppermute x3, waiting for transfers between devices, exchange(): got.append(lax.ppermute(own, ('frame', 'pix'), pairs))  2.31 us
    ppermute x1, starting transfers between devices, exchange(): lax.ppermute(got[0], 'pix', [(p, p ^ 1) for p in range(pix_count)])  1.66 us
    pallas_call x1, Pallas kernels, two_frames(): pl.pallas_call(functools.partial(late_kernel, pix_count, breadth), out_sh...  1.06 us
    pallas_call x1, Pallas kernels, two_frames(): pl.pallas_call(blank_kernel, out_shape=[jax.ShapeDtypeStruct(own.shape, o...  0.9 us
    unnamed x2, local copies, waits for them, and re-layouts  0.89 us
    ppermute x1, waiting for transfers between devices, exchange(): lax.ppermute(got[0], 'pix', [(p, p ^ 1) for p in range(pix_count)])  0.58 us
    pallas_call x1, Pallas kernels, two_frames(): pl.pallas_call(functools.partial(early_kernel, pix_count, breadth), out_s...  0.36 us
  transfers between devices with their start and end apart: 4, of which 2 were waited for; matrix products, arithmetic and copies ran while one was open for 0% of the time, Pallas kernels for 8%

profile of v2, /device:TPU:0, one launch (start us, length us, event | category | flops | bytes accessed | tf_op | source)
XLA Modules:
  0.0 16.5 jit_solution(14327541744342288915)
XLA Ops:
  0.6 5.0 %collective-permute-start = (bf16[192,256]{1,0:T(8,128)(2,1)}, bf16[192,256]{1,0:T(8,128)(2,1)S(1)}, u32[]{:S(2)}, u32[]{:S(2)}) collective-permute-start(bf16[192,256]{1,0:T(8,128)(2,1)} %bitcast.17), channel_id=1, source_target_pairs={{0,6},{1,4},{2,7},{3,5},{4,2},{5,0},{6,3},{7,1},{8,14},{9,12},{10,... | collective-permute-start | bytes 294920 | tf_op jit(solution)/shard_map/ppermute | solution.py:212
  5.7 0.5 %collective-permute-start.3 = (bf16[192,256]{1,0:T(8,128)(2,1)}, bf16[192,256]{1,0:T(8,128)(2,1)S(1)}, u32[]{:S(2)}, u32[]{:S(2)}) collective-permute-start(bf16[192,256]{1,0:T(8,128)(2,1)} %bitcast.18), channel_id=1, source_target_pairs={{0,4},{1,6},{2,5},{3,7},{4,0},{5,2},{6,1},{7,3},{8,12},{9,14},{10,... | collective-permute-start | bytes 294920 | tf_op jit(solution)/shard_map/ppermute | solution.py:212
  6.2 2.5 %collective-permute-start.2 = (bf16[192,256]{1,0:T(8,128)(2,1)}, bf16[192,256]{1,0:T(8,128)(2,1)S(1)}, u32[]{:S(2)}, u32[]{:S(2)}) collective-permute-start(bf16[192,256]{1,0:T(8,128)(2,1)} %bitcast.19), channel_id=1, source_target_pairs={{0,5},{1,7},{2,4},{3,6},{4,1},{5,3},{6,0},{7,2},{8,13},{9,15},{10,... | collective-permute-start | bytes 294920 | tf_op jit(solution)/shard_map/ppermute | solution.py:212
  8.7 0.0 collective-permute-done.refs_0_
  8.7 1.7 %collective-permute-start.1 = (bf16[192,256]{1,0:T(8,128)(2,1)S(1)}, bf16[192,256]{1,0:T(8,128)(2,1)S(1)}, u32[]{:S(2)}, u32[]{:S(2)}) collective-permute-start(bf16[192,256]{1,0:T(8,128)(2,1)S(1)} %collective-permute-done.refs_0_), channel_id=1, source_target_pairs={{0,1},{1,0},{2,3},{3,2},{4,5},{5,4},{6,7},{7,6},{8,9},{9,8},{10,11... | collective-permute-start | bytes 294920 | tf_op jit(solution)/shard_map/ppermute | solution.py:213
  10.4 0.0 copy-start
  10.4 0.9 %copy-done = bf16[1,2,96,256]{3,2,1,0:T(8,128)(2,1)S(1)} copy-done((bf16[1,2,96,256]{3,2,1,0:T(8,128)(2,1)S(1)}, bf16[1,2,96,256]{3,2,1,0:T(8,128)(2,1)}, u32[]{:S(2)}) %copy-start) | copy-done | bytes 98328
  11.3 0.9 %shard_map.78 = (bf16[192,256]{1,0:T(8,128)(2,1)S(1)}, bf16[2,96,768]{2,1,0:T(8,128)(2,1)}, bf16[2,96,192]{2,1,0:T(8,128)(2,1)}, bf16[2,48,96]{2,1,0:T(8,128)(2,...) custom-call(bf16[192,256]{1,0:T(8,128)(2,1)S(1)} %bitcast.20), custom_call_target="tpu_custom_call" | custom-call | flops 37748736 | bytes 589824 | tf_op jit(solution)/shard_map/pallas_call | solution.py:244
  12.2 0.0 collective-permute-done.3.refs_2_
  12.2 2.3 %collective-permute-done.2.refs_1_ = bf16[192,256]{1,0:T(8,128)(2,1)S(1)} collective-permute-done((bf16[192,256]{1,0:T(8,128)(2,1)}, bf16[192,256]{1,0:T(8,128)(2,1)S(1)}, u32[]{:S(2)}, u32[]{:S(2)}) %collective-permute-start.2) | collective-permute-done | bytes 98336 | tf_op jit(solution)/shard_map/ppermute | solution.py:212
  14.5 0.4 %shard_map.79 = (bf16[2,96,384]{2,1,0:T(8,128)(2,1)S(1)}, bf16[192,256]{1,0:T(8,128)(2,1)S(1)}, bf16[192,256]{1,0:T(8,128)(2,1)S(1)}, bf16[192,256]{1,0:T(8,128)...) custom-call(bf16[192,256]{1,0:T(8,128)(2,1)S(1)} %get-tuple-element.32.own_ref.refs_0_, ...), custom_call_target="tpu_custom_call" | custom-call | flops 75497472 | bytes 589824 | tf_op jit(solution)/shard_map/pallas_call | solution.py:254
  14.9 0.6 %collective-permute-done.1.refs_1_ = bf16[192,256]{1,0:T(8,128)(2,1)S(1)} collective-permute-done((bf16[192,256]{1,0:T(8,128)(2,1)S(1)}, bf16[192,256]{1,0:T(8,128)(2,1)S(1)}, u32[]{:S(2)}, u32[]{:S(2)}) %collective-permute-start.1) | collective-permute-done | bytes 98336 | tf_op jit(solution)/shard_map/ppermute | solution.py:213
  15.4 1.1 %shard_map.80 = (bf16[2,96,768]{2,1,0:T(8,128)(2,1)}, bf16[2,96,192]{2,1,0:T(8,128)(2,1)}, bf16[2,48,96]{2,1,0:T(8,128)(2,1)}, bf16[12,2,96]{2,1,0:T(2,128)(2,1)...) custom-call(bf16[192,256]{1,0:T(8,128)(2,1)S(1)} %get-tuple-element., ...), custom_call_target="tpu_custom_call", output_to_operand_aliasing={{0}: (9, {}), {1}: (10, {}), {2}: (11, {}), {3}: (12, {}), ... | custom-call | flops 75497472 | bytes 589824 | tf_op jit(solution)/shard_map/pallas_call | solution.py:275
Async XLA Ops:
  0.6 8.1 %collective-permute-start = (bf16[192,256]{1,0:T(8,128)(2,1)}, bf16[192,256]{1,0:T(8,128)(2,1)S(1)}, u32[]{:S(2)}, u32[]{:S(2)}) collective-permute-start(bf16[192,256]{1,0:T(8,128)(2,1)} %bitcast.17), channel_id=1, source_target_pairs={{0,6},{1,4},{2,7},{3,5},{4,2},{5,0},{6,3},{7,1},{8,14},{9,12},{10,... | collective-permute-start | bytes 294920 | tf_op jit(solution)/shard_map/ppermute | solution.py:212
  5.7 6.5 %collective-permute-start.3 = (bf16[192,256]{1,0:T(8,128)(2,1)}, bf16[192,256]{1,0:T(8,128)(2,1)S(1)}, u32[]{:S(2)}, u32[]{:S(2)}) collective-permute-start(bf16[192,256]{1,0:T(8,128)(2,1)} %bitcast.18), channel_id=1, source_target_pairs={{0,4},{1,6},{2,5},{3,7},{4,0},{5,2},{6,1},{7,3},{8,12},{9,14},{10,... | collective-permute-start | bytes 294920 | tf_op jit(solution)/shard_map/ppermute | solution.py:212
  6.2 8.3 %collective-permute-start.2 = (bf16[192,256]{1,0:T(8,128)(2,1)}, bf16[192,256]{1,0:T(8,128)(2,1)S(1)}, u32[]{:S(2)}, u32[]{:S(2)}) collective-permute-start(bf16[192,256]{1,0:T(8,128)(2,1)} %bitcast.19), channel_id=1, source_target_pairs={{0,5},{1,7},{2,4},{3,6},{4,1},{5,3},{6,0},{7,2},{8,13},{9,15},{10,... | collective-permute-start | bytes 294920 | tf_op jit(solution)/shard_map/ppermute | solution.py:212
  8.7 6.7 %collective-permute-start.1 = (bf16[192,256]{1,0:T(8,128)(2,1)S(1)}, bf16[192,256]{1,0:T(8,128)(2,1)S(1)}, u32[]{:S(2)}, u32[]{:S(2)}) collective-permute-start(bf16[192,256]{1,0:T(8,128)(2,1)S(1)} %collective-permute-done.refs_0_), channel_id=1, source_target_pairs={{0,1},{1,0},{2,3},{3,2},{4,5},{5,4},{6,7},{7,6},{8,9},{9,8},{10,11... | collective-permute-start | bytes 294920 | tf_op jit(solution)/shard_map/ppermute | solution.py:213
  10.4 0.9 %copy-start = (bf16[1,2,96,256]{3,2,1,0:T(8,128)(2,1)S(1)}, bf16[1,2,96,256]{3,2,1,0:T(8,128)(2,1)}, u32[]{:S(2)}) copy-start(bf16[1,2,96,256]{3,2,1,0:T(8,128)(2,1)} %param.1) | copy-start | bytes 294916

commit v3 on v1

--- a/solution.py
+++ b/solution.py
@@ -154,6 +154,11 @@
     odd = last % 2
     target[pl.ds(pl.multiple_of(odd * shard, shard), shard), :] = relayed_ref[...]
     target[pl.ds(pl.multiple_of((1 - odd) * shard, shard), shard), :] = partner_ref[...]
+    own = own_ref[...]
+    scores = (dot_nt(own, target[...]) * factor).astype(near_scores.dtype)
+    for r in range(2):
+        near_scores[r] = scores[r * breadth : (r + 1) * breadth, :]
+    send(0, 0, near_scores, forward, backward, sems, columns(near))
     level1 = level1_of(relayed_ref, summed, breadth)
     highs[...] = high_ref[...]
     lows[...] = low_ref[...]
@@ -164,26 +169,21 @@
     eighth = quarter // 2
     level3[...] = jnp.zeros_like(level3)
     level3[:eighth, :] = paired(level2[:quarter, :] + level2[quarter:, :], summed, quarter)
-    own = own_ref[...]
-    scores = (dot_nt(own, target[...]) * factor).astype(near_scores.dtype)
     halves = ((dot_nt(own, highs[...]) + dot_nt(own, lows[...])) * factor).astype(v1.dtype)
-    coarse = jnp.concatenate([*split(level2[...]), *split(level3[...])], axis=0)
+    high, low = split(jnp.concatenate([level2[...], level3[...]], axis=0))
     lines = []
     for r in range(2):
-        near_scores[r] = scores[r * breadth : (r + 1) * breadth, :]
         v1[r] = halves[r * breadth : (r + 1) * breadth, :]
-        product = dot_nt(coarse, own[r * breadth : (r + 1) * breadth, :]) * factor
-        v2[r] = (product[:half, :] + product[half:breadth, :]).astype(v2.dtype)
-        product = product[breadth:, :]
-        lines.append(product[:eighth, :] + product[level3.shape[0] : level3.shape[0] + eighth, :])
+        mine = own[r * breadth : (r + 1) * breadth, :]
+        product = (dot_nt(high, mine) + dot_nt(low, mine)) * factor
+        v2[r] = product[:half, :].astype(v2.dtype)
+        lines.append(product[half : half + eighth, :])
     v3[...] = jnp.stack(lines, axis=1).astype(v3.dtype)
-    pieces = ((0, 0, near_scores, columns(near)), (1, 1, v1, None), (2, 2, v2, None), (3, 3, v3, None))
 
     def start(targets):
         def run():
-            for level, piece, source, where in pieces:
-                target = targets[level] if where is None else targets[level].at[:, :, where]
-                pltpu.make_async_copy(source, target, sems.at[piece]).start()
+            for level, value in ((1, v1), (2, v2), (3, v3)):
+                pltpu.make_async_copy(value, targets[level], sems.at[level]).start()
 
         return run
 

time: 16.6 us -> 16.6 us (level)
  no operation moved by 1% of the time
where the time goes in v3:
time: 16.6 us; the launch traced here: 16.5 us
  starting transfers between devices  9.74 us (59%)
  waiting for transfers between devices  2.92 us (18%)
  Pallas kernels  2.27 us (14%)
  local copies, waits for them, and re-layouts  0.89 us (5%)
  between operations  0.66 us (4%)
    ppermute x3, starting transfers between devices, exchange(): got.append(lax.ppermute(own, ('frame', 'pix'), pairs))  8.08 us
    ppermute x3, waiting for transfers between devices, exchange(): got.append(lax.ppermute(own, ('frame', 'pix'), pairs))  2.31 us
    ppermute x1, starting transfers between devices, exchange(): lax.ppermute(got[0], 'pix', [(p, p ^ 1) for p in range(pix_count)])  1.66 us
    pallas_call x1, Pallas kernels, two_frames(): pl.pallas_call(functools.partial(late_kernel, pix_count, breadth), out_sh...  1.05 us
    pallas_call x1, Pallas kernels, two_frames(): pl.pallas_call(blank_kernel, out_shape=[jax.ShapeDtypeStruct(own.shape, o...  0.9 us
    unnamed x2, local copies, waits for them, and re-layouts  0.89 us
    ppermute x1, waiting for transfers between devices, exchange(): lax.ppermute(got[0], 'pix', [(p, p ^ 1) for p in range(pix_count)])  0.62 us
  transfers between devices with their start and end apart: 4, of which 2 were waited for; matrix products, arithmetic and copies ran while one was open for 0% of the time, Pallas kernels for 7%

profile of v3, /device:TPU:0, one launch (start us, length us, event | category | flops | bytes accessed | tf_op | source)
XLA Modules:
  0.0 16.5 jit_solution(16497129401256065785)
XLA Ops:
  0.6 5.0 %collective-permute-start = (bf16[192,256]{1,0:T(8,128)(2,1)}, bf16[192,256]{1,0:T(8,128)(2,1)S(1)}, u32[]{:S(2)}, u32[]{:S(2)}) collective-permute-start(bf16[192,256]{1,0:T(8,128)(2,1)} %bitcast.17), channel_id=1, source_target_pairs={{0,6},{1,4},{2,7},{3,5},{4,2},{5,0},{6,3},{7,1},{8,14},{9,12},{10,... | collective-permute-start | bytes 294920 | tf_op jit(solution)/shard_map/ppermute | solution.py:209
  5.7 0.5 %collective-permute-start.3 = (bf16[192,256]{1,0:T(8,128)(2,1)}, bf16[192,256]{1,0:T(8,128)(2,1)S(1)}, u32[]{:S(2)}, u32[]{:S(2)}) collective-permute-start(bf16[192,256]{1,0:T(8,128)(2,1)} %bitcast.18), channel_id=1, source_target_pairs={{0,4},{1,6},{2,5},{3,7},{4,0},{5,2},{6,1},{7,3},{8,12},{9,14},{10,... | collective-permute-start | bytes 294920 | tf_op jit(solution)/shard_map/ppermute | solution.py:209
  6.2 2.5 %collective-permute-start.2 = (bf16[192,256]{1,0:T(8,128)(2,1)}, bf16[192,256]{1,0:T(8,128)(2,1)S(1)}, u32[]{:S(2)}, u32[]{:S(2)}) collective-permute-start(bf16[192,256]{1,0:T(8,128)(2,1)} %bitcast.19), channel_id=1, source_target_pairs={{0,5},{1,7},{2,4},{3,6},{4,1},{5,3},{6,0},{7,2},{8,13},{9,15},{10,... | collective-permute-start | bytes 294920 | tf_op jit(solution)/shard_map/ppermute | solution.py:209
  8.7 0.0 collective-permute-done.refs_0_
  8.7 1.7 %collective-permute-start.1 = (bf16[192,256]{1,0:T(8,128)(2,1)S(1)}, bf16[192,256]{1,0:T(8,128)(2,1)S(1)}, u32[]{:S(2)}, u32[]{:S(2)}) collective-permute-start(bf16[192,256]{1,0:T(8,128)(2,1)S(1)} %collective-permute-done.refs_0_), channel_id=1, source_target_pairs={{0,1},{1,0},{2,3},{3,2},{4,5},{5,4},{6,7},{7,6},{8,9},{9,8},{10,11... | collective-permute-start | bytes 294920 | tf_op jit(solution)/shard_map/ppermute | solution.py:210
  10.4 0.0 copy-start
  10.4 0.9 %copy-done = bf16[1,2,96,256]{3,2,1,0:T(8,128)(2,1)S(1)} copy-done((bf16[1,2,96,256]{3,2,1,0:T(8,128)(2,1)S(1)}, bf16[1,2,96,256]{3,2,1,0:T(8,128)(2,1)}, u32[]{:S(2)}) %copy-start) | copy-done | bytes 98328
  11.3 0.9 %shard_map.78 = (bf16[192,256]{1,0:T(8,128)(2,1)S(1)}, bf16[2,96,768]{2,1,0:T(8,128)(2,1)}, bf16[2,96,192]{2,1,0:T(8,128)(2,1)}, bf16[2,48,96]{2,1,0:T(8,128)(2,...) custom-call(bf16[192,256]{1,0:T(8,128)(2,1)S(1)} %bitcast.20), custom_call_target="tpu_custom_call" | custom-call | flops 37748736 | bytes 589824 | tf_op jit(solution)/shard_map/pallas_call | solution.py:241
  12.2 0.0 collective-permute-done.3.refs_2_
  12.2 2.3 %collective-permute-done.2.refs_1_ = bf16[192,256]{1,0:T(8,128)(2,1)S(1)} collective-permute-done((bf16[192,256]{1,0:T(8,128)(2,1)}, bf16[192,256]{1,0:T(8,128)(2,1)S(1)}, u32[]{:S(2)}, u32[]{:S(2)}) %collective-permute-start.2) | collective-permute-done | bytes 98336 | tf_op jit(solution)/shard_map/ppermute | solution.py:209
  14.5 0.3 %shard_map.79 = (bf16[2,96,384]{2,1,0:T(8,128)(2,1)S(1)}, bf16[192,256]{1,0:T(8,128)(2,1)S(1)}, bf16[192,256]{1,0:T(8,128)(2,1)S(1)}, bf16[192,256]{1,0:T(8,128)...) custom-call(bf16[192,256]{1,0:T(8,128)(2,1)S(1)} %get-tuple-element.31.own_ref.refs_0_, ...), custom_call_target="tpu_custom_call" | custom-call | flops 75497472 | bytes 589824 | tf_op jit(solution)/shard_map/pallas_call | solution.py:251
  14.8 0.6 %collective-permute-done.1.refs_1_ = bf16[192,256]{1,0:T(8,128)(2,1)S(1)} collective-permute-done((bf16[192,256]{1,0:T(8,128)(2,1)S(1)}, bf16[192,256]{1,0:T(8,128)(2,1)S(1)}, u32[]{:S(2)}, u32[]{:S(2)}) %collective-permute-start.1) | collective-permute-done | bytes 98336 | tf_op jit(solution)/shard_map/ppermute | solution.py:210
  15.4 1.0 %shard_map.80 = (bf16[2,96,768]{2,1,0:T(8,128)(2,1)}, bf16[2,96,192]{2,1,0:T(8,128)(2,1)}, bf16[2,48,96]{2,1,0:T(8,128)(2,1)}, bf16[12,2,96]{2,1,0:T(2,128)(2,1)...) custom-call(bf16[192,256]{1,0:T(8,128)(2,1)S(1)} %get-tuple-element., ...), custom_call_target="tpu_custom_call", output_to_operand_aliasing={{0}: (8, {}), {1}: (9, {}), {2}: (10, {}), {3}: (11, {}), {... | custom-call | flops 75497472 | bytes 589824 | tf_op jit(solution)/shard_map/pallas_call | solution.py:271
Async XLA Ops:
  0.6 8.1 %collective-permute-start = (bf16[192,256]{1,0:T(8,128)(2,1)}, bf16[192,256]{1,0:T(8,128)(2,1)S(1)}, u32[]{:S(2)}, u32[]{:S(2)}) collective-permute-start(bf16[192,256]{1,0:T(8,128)(2,1)} %bitcast.17), channel_id=1, source_target_pairs={{0,6},{1,4},{2,7},{3,5},{4,2},{5,0},{6,3},{7,1},{8,14},{9,12},{10,... | collective-permute-start | bytes 294920 | tf_op jit(solution)/shard_map/ppermute | solution.py:209
  5.7 6.5 %collective-permute-start.3 = (bf16[192,256]{1,0:T(8,128)(2,1)}, bf16[192,256]{1,0:T(8,128)(2,1)S(1)}, u32[]{:S(2)}, u32[]{:S(2)}) collective-permute-start(bf16[192,256]{1,0:T(8,128)(2,1)} %bitcast.18), channel_id=1, source_target_pairs={{0,4},{1,6},{2,5},{3,7},{4,0},{5,2},{6,1},{7,3},{8,12},{9,14},{10,... | collective-permute-start | bytes 294920 | tf_op jit(solution)/shard_map/ppermute | solution.py:209
  6.2 8.3 %collective-permute-start.2 = (bf16[192,256]{1,0:T(8,128)(2,1)}, bf16[192,256]{1,0:T(8,128)(2,1)S(1)}, u32[]{:S(2)}, u32[]{:S(2)}) collective-permute-start(bf16[192,256]{1,0:T(8,128)(2,1)} %bitcast.19), channel_id=1, source_target_pairs={{0,5},{1,7},{2,4},{3,6},{4,1},{5,3},{6,0},{7,2},{8,13},{9,15},{10,... | collective-permute-start | bytes 294920 | tf_op jit(solution)/shard_map/ppermute | solution.py:209
  8.7 6.7 %collective-permute-start.1 = (bf16[192,256]{1,0:T(8,128)(2,1)S(1)}, bf16[192,256]{1,0:T(8,128)(2,1)S(1)}, u32[]{:S(2)}, u32[]{:S(2)}) collective-permute-start(bf16[192,256]{1,0:T(8,128)(2,1)S(1)} %collective-permute-done.refs_0_), channel_id=1, source_target_pairs={{0,1},{1,0},{2,3},{3,2},{4,5},{5,4},{6,7},{7,6},{8,9},{9,8},{10,11... | collective-permute-start | bytes 294920 | tf_op jit(solution)/shard_map/ppermute | solution.py:210
  10.4 0.9 %copy-start = (bf16[1,2,96,256]{3,2,1,0:T(8,128)(2,1)S(1)}, bf16[1,2,96,256]{3,2,1,0:T(8,128)(2,1)}, u32[]{:S(2)}) copy-start(bf16[1,2,96,256]{3,2,1,0:T(8,128)(2,1)} %param.1) | copy-start | bytes 294916
